TPU v7x, 32 devices: a whole 2x2x4 slice. The times are simulated.
32 devices in a mesh: grp: 8 (over y, x, core), sp: 4 (over z).
Axes of the slice: x: 2, y: 2, z: 4, core: 2. Of those that a mesh axis runs over, the one named last changes fastest.
Arguments:
- latents: bfloat16 [8, 512, 3072], P('grp', 'sp'), may hold values from -6 to 6
- timestep: int32 [8], P('grp'), may hold values from 0 to 999
- w_mod: bfloat16 [256, 9216], replicated, may hold values from -0.375 to 0.375
- w_qkv: bfloat16 [4, 3072, 384], P('sp', 'grp'), may hold values from -2 to 2
- w_out: bfloat16 [4, 128, 3072], P('sp', 'grp'), may hold values from -0.5 to 0.5
Outputs:
- update: bfloat16 [8, 512, 3072], P('grp', 'sp')
All inputs are finite; a program needn't handle non-finite values.
Results may differ from a plain program's by a relative error of at most 0.012.
Values may be sent and summed in bfloat16 or wider, within the bound.
No kernel may reach another device: no remote copies, remote signals or barrier semaphores. Data moves between devices by JAX's collectives and lax.ppermute only.
A program may use at most 128 MiB of HBM per device.

v0:
```python
import functools
import math

import jax
import jax.numpy as jnp
from jax import lax
from jax.experimental import pallas as pl
from jax.experimental.pallas import tpu as pltpu
from jax.sharding import PartitionSpec as P


AXES = ("grp", "sp")


def modulation(timestep, w_mod):
    half_freq = w_mod.shape[0] // 2
    freqs = jnp.exp(-math.log(10000.0) * jnp.arange(half_freq, dtype=jnp.float32) / half_freq)
    angles = timestep.astype(jnp.float32)[:, None] * freqs[None, :]
    embed = jnp.concatenate([jnp.cos(angles), jnp.sin(angles)], axis=1).astype(jnp.bfloat16)
    return jnp.dot(embed, w_mod, preferred_element_type=jnp.float32)


def normalize_kernel(block, x_ref, shift_ref, scale_ref, out_ref):
    gain = 1.0 + scale_ref[...]
    shift = shift_ref[...]

    @pl.loop(0, x_ref.shape[0] // block)
    def _(step):
        rows = pl.ds(pl.multiple_of(step * block, block), block)
        values = x_ref[rows, :].astype(jnp.float32)
        centered = values - jnp.mean(values, axis=-1, keepdims=True)
        spread = jnp.mean(centered * centered, axis=-1, keepdims=True)
        out_ref[rows, :] = (centered * lax.rsqrt(spread + 1e-06) * gain + shift).astype(out_ref.dtype)


def normalize(rows, shift, scale):
    vmem = pl.BlockSpec(memory_space=pltpu.VMEM)
    block = math.gcd(rows.shape[0], 32)
    return pl.pallas_call(
        functools.partial(normalize_kernel, block),
        out_shape=jax.ShapeDtypeStruct(rows.shape, jnp.bfloat16),
        in_specs=[vmem] * 3,
        out_specs=vmem,
        compiler_params=pltpu.CompilerParams(vmem_limit_bytes=8 * 2**20),
        cost_estimate=pl.CostEstimate(
            flops=10 * rows.size, bytes_accessed=4 * rows.size, transcendentals=0
        ),
    )(rows, shift, scale)


def project_kernel(chunks, owner_ref, reorder_ref, *refs):
    xs, pieces, (query_ref, kv_ref) = refs[:chunks], refs[chunks:-2], refs[-2:]
    head_size = query_ref.shape[1]
    tokens = xs[0].shape[0]
    for chunk, x_ref in enumerate(xs):
        total = jnp.zeros((tokens, 3 * head_size), jnp.float32)
        for index, piece in enumerate(pieces):
            rows = piece.shape[0]
            start = pl.multiple_of(owner_ref[index] * rows, 128)
            total += jnp.dot(x_ref[:, pl.ds(start, rows)], piece[...], preferred_element_type=jnp.float32)
        qkv = total.astype(jnp.bfloat16)
        values = jnp.dot(qkv[:, 2 * head_size :], reorder_ref[...], preferred_element_type=jnp.float32)
        place = pl.ds(chunk * tokens, tokens)
        query_ref[place, :] = qkv[:, :head_size]
        kv_ref[place, :head_size] = qkv[:, head_size : 2 * head_size]
        kv_ref[place, head_size:] = values.astype(jnp.bfloat16)


def project(xs, pieces, owners, reorder):
    rows, columns = pieces[0].shape
    head_size = columns // 3
    if rows % 128:
        x = jnp.concatenate(xs, axis=0)
        total = jnp.zeros((x.shape[0], columns), jnp.float32)
        for index, piece in enumerate(pieces):
            part = lax.dynamic_slice_in_dim(x, owners[index] * rows, rows, axis=1)
            total += jnp.dot(part, piece, preferred_element_type=jnp.float32)
        qkv = total.astype(jnp.bfloat16)
        values = jnp.dot(qkv[:, 2 * head_size :], reorder, preferred_element_type=jnp.float32)
        kv = jnp.concatenate([qkv[:, head_size : 2 * head_size], values.astype(jnp.bfloat16)], axis=1)
        return qkv[:, :head_size], kv
    vmem = pl.BlockSpec(memory_space=pltpu.VMEM)
    tokens = sum(x.shape[0] for x in xs)
    return pl.pallas_call(
        functools.partial(project_kernel, len(xs)),
        out_shape=(
            jax.ShapeDtypeStruct((tokens, head_size), jnp.bfloat16),
            jax.ShapeDtypeStruct((tokens, 2 * head_size), jnp.bfloat16),
        ),
        in_specs=[pl.BlockSpec(memory_space=pltpu.SMEM)] + [vmem] * (1 + len(xs) + len(pieces)),
        out_specs=(vmem, vmem),
        compiler_params=pltpu.CompilerParams(vmem_limit_bytes=16 * 2**20),
        cost_estimate=pl.CostEstimate(
            flops=2 * tokens * xs[0].shape[1] * columns,
            bytes_accessed=2 * (tokens + columns) * xs[0].shape[1],
            transcendentals=0,
        ),
    )(owners, reorder, *xs, *pieces)


def after(value, *ready):
    return lax.optimization_barrier((value,) + ready)[0]


def attend(query, keys, values):
    head_size = query.shape[1]
    scores = lax.dot_general(query, keys, (((1,), (1,)), ((), ())), preferred_element_type=jnp.float32)
    scores = scores / math.sqrt(head_size)
    largest = jnp.max(scores, axis=1, keepdims=True)
    weights = jnp.exp(scores - largest)
    probs = (weights / jnp.sum(weights, axis=1, keepdims=True)).astype(jnp.bfloat16)
    return jnp.dot(probs, values, preferred_element_type=jnp.float32).astype(jnp.bfloat16)


def on_device(groups, spread, latents, timestep, w_mod, w_qkv, w_out):
    _, tok_local, width = latents.shape
    head_size = w_qkv.shape[2] // 3
    half = spread // 2
    chips = groups // 2
    grp = lax.axis_index("grp")

    def move(value, grp_to, sp_to):
        pairs = []
        for g in range(groups):
            for s in range(spread):
                pairs.append((g * spread + s, grp_to(g) * spread + sp_to(s)))
        return lax.ppermute(value, AXES, pairs)

    def sp_shift(across, along):
        def to(s):
            return (s // half + across) % 2 * half + (s % half + along) % half

        return to

    def chip_step(step):
        if chips & (chips - 1) == 0:
            return lambda g: ((g // 2) ^ step) * 2 + g % 2
        return lambda g: (g // 2 - step) % chips * 2 + g % 2

    def chip_owner(step):
        if chips & (chips - 1) == 0:
            return (grp // 2) ^ step
        return (grp // 2 + step) % chips

    same = lambda index: index
    partner = lambda g: g ^ 1

    def over_chips(value):
        return [value] + [move(value, chip_step(step), same) for step in range(1, chips)]

    def over_cores(pieces):
        return pieces + [move(piece, partner, same) for piece in pieces]

    owners = jnp.stack(
        [chip_owner(step) * 2 + (grp % 2 + flip) % 2 for flip in range(2) for step in range(chips)]
    ).astype(jnp.int32)

    rows_each = head_size // groups
    column = jnp.arange(head_size, dtype=jnp.int32)
    source = jnp.repeat(owners, rows_each) * rows_each + column % rows_each
    reorder = (column[:, None] == source[None, :]).astype(jnp.bfloat16)

    other_shard = move(w_qkv[0], same, sp_shift(1, 0))
    own_in = over_chips(w_qkv[0])
    out_shards = []
    for step in range(half):
        for across in range(2):
            shard = w_out[0]
            if step or across:
                shard = move(shard, same, sp_shift(across, step))
            out_shards.append(shard)
    raw = [move(latents[0], same, sp_shift(0, -step)) for step in range(1, half)]

    mod = modulation(timestep, w_mod)
    shift, scale, gate = mod[:, :width], mod[:, width : 2 * width], mod[:, 2 * width :]
    mine_normed = normalize(latents[0], shift, scale)

    other_in = over_chips(after(other_shard, mine_normed))
    own_pieces = over_cores(own_in)
    out_mine = over_chips(after(jnp.stack(out_shards), mine_normed))
    query_own, kv_own = project([mine_normed], own_pieces, owners, reorder)
    other_pieces = over_cores(after(other_in, kv_own))

    queries, local_kv, remote_kv = [[], []], [], []
    for stage in range(2):
        if stage:
            raw = after(raw, local_kv[0])
            xs = [normalize(rows, shift, scale) for rows in raw]
            query_own, kv_own = project(xs, own_pieces, owners, reorder)
        else:
            xs = [mine_normed]
        query_other, kv_other = project(xs, other_pieces, owners, reorder)
        queries[0].append(query_own)
        queries[1].append(query_other)
        local_kv.append(jnp.concatenate([kv_own, kv_other], axis=1))
        remote_kv.append(move(local_kv[-1], same, sp_shift(1, 0)))
    heads = []
    for index in range(2):
        here = index * 2 * head_size
        there = (1 - index) * 2 * head_size
        keys = [kv[:, here : here + head_size] for kv in local_kv]
        keys += [kv[:, there : there + head_size] for kv in remote_kv]
        values = [kv[:, here + head_size : here + 2 * head_size] for kv in local_kv]
        values += [kv[:, there + head_size : there + 2 * head_size] for kv in remote_kv]
        heads.append(
            attend(
                jnp.concatenate(queries[index], axis=0),
                jnp.concatenate(keys, axis=0),
                jnp.concatenate(values, axis=0),
            )
        )
    both = jnp.concatenate(heads, axis=1)

    mine = []
    for step in range(half):
        part = both[step * tok_local : (step + 1) * tok_local]
        if step:
            part = move(part, same, sp_shift(0, step))
        mine.append(part)
    out_pieces = over_cores(after(out_mine, both))
    attended = jnp.concatenate(mine, axis=1)
    rows = jnp.concatenate(out_pieces, axis=1).reshape(attended.shape[1], width)
    total = jnp.dot(attended, rows, preferred_element_type=jnp.float32)
    return (gate * total).astype(jnp.bfloat16)[None]


def solution(mesh):
    placed = (P("grp", "sp", None), P("grp"), P(), P("sp", "grp", None), P("sp", "grp", None))

    def body(*args):
        return on_device(mesh.shape["grp"], mesh.shape["sp"], *args)

    return jax.shard_map(
        body, mesh=mesh, in_specs=placed, out_specs=P("grp", "sp", None), check_vma=False
    )
```

profile of v0, /device:TPU:0, one launch (start us, length us, event | category | flops | bytes accessed | tf_op | source)
XLA Modules:
  0.0 90.1 jit_solution(6160047666053598076)
XLA Ops:
  0.0 3.0 %collective-permute-start = (bf16[384,384]{1,0:T(8,128)(2,1)}, bf16[384,384]{1,0:T(8,128)(2,1)S(1)}, u32[]{:S(2)}, u32[]{:S(2)}) collective-permute-start(bf16[384,384]{1,0:T(8,128)(2,1)} %bitcast.23), channel_id=1, source_target_pairs={{0,8},{1,9},{2,10},{3,11},{4,12},{5,13},{6,14},{7,15},{8,0},{9,1},... | collective-permute-start | bytes 884744 | tf_op jit(solution)/shard_map/ppermute | solution.py:127
  3.0 1.5 %collective-permute-start.1 = (bf16[384,384]{1,0:T(8,128)(2,1)}, bf16[384,384]{1,0:T(8,128)(2,1)S(1)}, u32[]{:S(2)}, u32[]{:S(2)}) collective-permute-start(bf16[384,384]{1,0:T(8,128)(2,1)} %bitcast.24), channel_id=1, source_target_pairs={{0,16},{1,17},{2,18},{3,19},{4,20},{5,21},{6,22},{7,23},{8,24},{9,... | collective-permute-start | bytes 884744 | tf_op jit(solution)/shard_map/ppermute | solution.py:127
  4.5 2.6 %collective-permute-start.19 = (bf16[16,3072]{1,0:T(8,128)(2,1)}, bf16[16,3072]{1,0:T(8,128)(2,1)S(1)}, u32[]{:S(2)}, u32[]{:S(2)}) collective-permute-start(bf16[16,3072]{1,0:T(8,128)(2,1)} %bitcast.33), channel_id=1, source_target_pairs={{0,2},{1,3},{2,0},{3,1},{4,6},{5,7},{6,4},{7,5},{8,10},{9,11},{10,... | collective-permute-start | bytes 294920 | tf_op jit(solution)/shard_map/ppermute | solution.py:127
  7.1 1.6 %collective-permute-start.20 = (bf16[16,3072]{1,0:T(8,128)(2,1)}, bf16[16,3072]{1,0:T(8,128)(2,1)S(1)}, u32[]{:S(2)}, u32[]{:S(2)}) collective-permute-start(bf16[16,3072]{1,0:T(8,128)(2,1)} %bitcast.34), channel_id=1, source_target_pairs={{0,1},{1,0},{2,3},{3,2},{4,5},{5,4},{6,7},{7,6},{8,9},{9,8},{10,11... | collective-permute-start | bytes 294920 | tf_op jit(solution)/shard_map/ppermute | solution.py:127
  8.7 0.2 collective-permute-start.21
  9.6 3.1 %fusion.59 = f32[1,9216]{1,0:T(1,128)S(1)} fusion(bf16[256,1]{0,1:T(2,128)(2,1)S(1)} %reshape.45, bf16[256,9216]{1,0:T(8,128)(2,1)} %param.7), kind=kOutput, calls=%fused_computation.92 | convolution fusion | flops 4718592 | bytes 4755968 | tf_op jit(solution)/shard_map/dot_general | solution.py:20
  13.0 1.1 %shard_map.55.refs_0_ = bf16[128,3072]{1,0:T(8,128)(2,1)S(1)} custom-call(bf16[128,3072]{1,0:T(8,128)(2,1)S(1)} %bitcast.30, f32[1,3072]{1,0:T(1,128)S(1)} %get-tuple-element.62.shift_ref, f32[1,3072]{1,0:T(1,128)S(1)} %get-tuple-element.63.scale_ref), custom_call_target="tpu_custom_call" | custom-call | flops 3932160 | bytes 1572864 | tf_op jit(solution)/shard_map/pallas_call | solution.py:39
  14.2 1.8 %collective-permute-start.8 = (bf16[384,384]{1,0:T(8,128)(2,1)S(1)}, bf16[384,384]{1,0:T(8,128)(2,1)S(1)}, u32[]{:S(2)}, u32[]{:S(2)}) collective-permute-start(bf16[384,384]{1,0:T(8,128)(2,1)S(1)} %bitcast.25), channel_id=1, source_target_pairs={{0,2},{1,3},{2,0},{3,1},{4,6},{5,7},{6,4},{7,5},{8,10},{9,11},{10,... | collective-permute-start | bytes 884744 | tf_op jit(solution)/shard_map/ppermute | solution.py:127
  16.0 0.6 collective-permute-start.22
  16.6 0.5 collective-permute-start.23
  17.1 11.8 %collective-permute-done.8.refs_1_ = bf16[384,384]{1,0:T(8,128)(2,1)S(1)} collective-permute-done((bf16[384,384]{1,0:T(8,128)(2,1)S(1)}, bf16[384,384]{1,0:T(8,128)(2,1)S(1)}, u32[]{:S(2)}, u32[]{:S(2)}) %collective-permute-start.8) | collective-permute-done | bytes 294944 | tf_op jit(solution)/shard_map/ppermute | solution.py:127
  28.9 0.5 collective-permute-start.24
  29.4 2.5 %collective-permute-start.2 = (bf16[384,384]{1,0:T(8,128)(2,1)S(1)}, bf16[384,384]{1,0:T(8,128)(2,1)S(1)}, u32[]{:S(2)}, u32[]{:S(2)}) collective-permute-start(bf16[384,384]{1,0:T(8,128)(2,1)S(1)} %bitcast.26), channel_id=1, source_target_pairs={{0,24},{1,25},{2,26},{3,27},{4,28},{5,29},{6,30},{7,31},{8,16},{9,... | collective-permute-start | bytes 884744 | tf_op jit(solution)/shard_map/ppermute | solution.py:127
  31.9 0.4 collective-permute-start.7
  32.3 0.2 collective-permute-start.4
  32.5 9.3 %collective-permute-done.24 = bf16[4,16,3072]{2,1,0:T(8,128)(2,1)S(1)} collective-permute-done((bf16[4,16,3072]{2,1,0:T(8,128)(2,1)S(1)}, bf16[4,16,3072]{2,1,0:T(8,128)(2,1)S(1)}, u32[]{:S(2)}, u32[]{:S(2)}) %collective-permute-start.24) | collective-permute-done | bytes 393248 | tf_op jit(solution)/shard_map/ppermute | solution.py:127
  41.9 4.4 %collective-permute-done.2.refs_4_ = bf16[384,384]{1,0:T(8,128)(2,1)S(1)} collective-permute-done((bf16[384,384]{1,0:T(8,128)(2,1)S(1)}, bf16[384,384]{1,0:T(8,128)(2,1)S(1)}, u32[]{:S(2)}, u32[]{:S(2)}) %collective-permute-start.2) | collective-permute-done | bytes 294944 | tf_op jit(solution)/shard_map/ppermute | solution.py:127
  46.2 0.5 collective-permute-start.10
  46.7 1.5 %collective-permute-start.11 = (bf16[384,384]{1,0:T(8,128)(2,1)S(1)}, bf16[384,384]{1,0:T(8,128)(2,1)S(1)}, u32[]{:S(2)}, u32[]{:S(2)}) collective-permute-start(bf16[384,384]{1,0:T(8,128)(2,1)S(1)} %collective-permute-done.8.refs_1_), channel_id=1, source_target_pairs={{0,24},{1,25},{2,26},{3,27},{4,28},{5,29},{6,30},{7,31},{8,16},{9,... | collective-permute-start | bytes 884744 | tf_op jit(solution)/shard_map/ppermute | solution.py:127
  48.2 1.5 %collective-permute-start.9 = (bf16[384,384]{1,0:T(8,128)(2,1)S(1)}, bf16[384,384]{1,0:T(8,128)(2,1)S(1)}, u32[]{:S(2)}, u32[]{:S(2)}) collective-permute-start(bf16[384,384]{1,0:T(8,128)(2,1)S(1)} %collective-permute-done.8.refs_1_), channel_id=1, source_target_pairs={{0,8},{1,9},{2,10},{3,11},{4,12},{5,13},{6,14},{7,15},{8,0},{9,1},... | collective-permute-start | bytes 884744 | tf_op jit(solution)/shard_map/ppermute | solution.py:127
  49.7 1.5 %collective-permute-done.6.refs_8_ = bf16[384,384]{1,0:T(8,128)(2,1)S(1)} collective-permute-done((bf16[384,384]{1,0:T(8,128)(2,1)S(1)}, bf16[384,384]{1,0:T(8,128)(2,1)S(1)}, u32[]{:S(2)}, u32[]{:S(2)}) %collective-permute-start.6) | collective-permute-done | bytes 294944 | tf_op jit(solution)/shard_map/ppermute | solution.py:127
  51.3 1.3 %shard_map.56 = (bf16[128,128]{1,0:T(8,128)(2,1)S(1)}, bf16[128,256]{1,0:T(8,128)(2,1)S(1)}) custom-call(s32[8]{0:T(128)S(1)} %stack.47.owner_ref, bf16[128,128]{1,0:T(8,128)(2,1)S(1)} %fusion.43.reorder_ref, bf16[128,3072]{1,0:T(8,128)(2,1)S(1)} %shard_map.55.refs_0_, bf16[384,384]{1,0:T(8,128)(2,1)S(1)} %bitcast.28, ...), custom_call_target="tpu_custom_call" | custom-call | flops 301989888 | bytes 3145728 | tf_op jit(solution)/shard_map/pallas_call | solution.py:84
  52.6 7.1 %collective-permute-done.10.refs_3_ = bf16[384,384]{1,0:T(8,128)(2,1)S(1)} collective-permute-done((bf16[384,384]{1,0:T(8,128)(2,1)S(1)}, bf16[384,384]{1,0:T(8,128)(2,1)S(1)}, u32[]{:S(2)}, u32[]{:S(2)}) %collective-permute-start.10) | collective-permute-done | bytes 294944 | tf_op jit(solution)/shard_map/ppermute | solution.py:127
  59.7 1.2 %collective-permute-done.9.refs_2_ = bf16[384,384]{1,0:T(8,128)(2,1)S(1)} collective-permute-done((bf16[384,384]{1,0:T(8,128)(2,1)S(1)}, bf16[384,384]{1,0:T(8,128)(2,1)S(1)}, u32[]{:S(2)}, u32[]{:S(2)}) %collective-permute-start.9) | collective-permute-done | bytes 294944 | tf_op jit(solution)/shard_map/ppermute | solution.py:127
  60.9 0.5 collective-permute-start.13
  61.5 0.5 collective-permute-start.15
  62.0 0.5 collective-permute-done.12.refs_5_
  62.5 0.1 collective-permute-start.25
  62.7 0.3 collective-permute-done.13.refs_6_
  62.9 0.1 collective-permute-start.26
  63.1 0.3 collective-permute-done.14.refs_7_
  63.4 0.1 collective-permute-start.27
  63.5 0.3 collective-permute-done.15.refs_8_
  63.8 0.1 collective-permute-start.28
  63.9 1.3 %shard_map.57 = (bf16[128,128]{1,0:T(8,128)(2,1)S(1)}, bf16[128,256]{1,0:T(8,128)(2,1)S(1)}) custom-call(s32[8]{0:T(128)S(1)} %stack.47.owner_ref, bf16[128,128]{1,0:T(8,128)(2,1)S(1)} %fusion.43.reorder_ref, bf16[128,3072]{1,0:T(8,128)(2,1)S(1)} %shard_map.55.refs_0_, bf16[384,384]{1,0:T(8,128)(2,1)S(1)} %collective-permute-done.8.refs_1_, ...), custom_call_target="tpu_custom_call" | custom-call | flops 301989888 | bytes 3145728 | tf_op jit(solution)/shard_map/pallas_call | solution.py:84
  65.3 4.8 %collective-permute-start.16 = (bf16[128,512]{1,0:T(8,128)(2,1)S(1)}, bf16[128,512]{1,0:T(8,128)(2,1)S(1)}, u32[]{:S(2)}, u32[]{:S(2)}) collective-permute-start(bf16[128,512]{1,0:T(8,128)(2,1)S(1)} %constant_dynamic-update-slice_fusion), channel_id=1, source_target_pairs={{0,2},{1,3},{2,0},{3,1},{4,6},{5,7},{6,4},{7,5},{8,10},{9,11},{10,... | collective-permute-start | bytes 393224 | tf_op jit(solution)/shard_map/ppermute | solution.py:127
  70.1 1.1 %shard_map.58.refs_0_ = bf16[128,3072]{1,0:T(8,128)(2,1)S(1)} custom-call(bf16[128,3072]{1,0:T(8,128)(2,1)S(1)} %collective-permute-done.7.x_ref, f32[1,3072]{1,0:T(1,128)S(1)} %get-tuple-element.62.shift_ref, f32[1,3072]{1,0:T(1,128)S(1)} %get-tuple-element.63.scale_ref), custom_call_target="tpu_custom_call" | custom-call | flops 3932160 | bytes 1572864 | tf_op jit(solution)/shard_map/pallas_call | solution.py:39
  71.2 1.3 %shard_map.59 = (bf16[128,128]{1,0:T(8,128)(2,1)S(1)}, bf16[128,256]{1,0:T(8,128)(2,1)S(1)}) custom-call(s32[8]{0:T(128)S(1)} %stack.47.owner_ref, bf16[128,128]{1,0:T(8,128)(2,1)S(1)} %fusion.43.reorder_ref, bf16[128,3072]{1,0:T(8,128)(2,1)S(1)} %shard_map.58.refs_0_, bf16[384,384]{1,0:T(8,128)(2,1)S(1)} %bitcast.29, ...), custom_call_target="tpu_custom_call" | custom-call | flops 301989888 | bytes 3145728 | tf_op jit(solution)/shard_map/pallas_call | solution.py:84
  72.5 1.3 %shard_map.60 = (bf16[128,128]{1,0:T(8,128)(2,1)S(1)}, bf16[128,256]{1,0:T(8,128)(2,1)S(1)}) custom-call(s32[8]{0:T(128)S(1)} %stack.47.owner_ref, bf16[128,128]{1,0:T(8,128)(2,1)S(1)} %fusion.43.reorder_ref, bf16[128,3072]{1,0:T(8,128)(2,1)S(1)} %shard_map.58.refs_0_, bf16[384,384]{1,0:T(8,128)(2,1)S(1)} %collective-permute-done.8.refs_1_, ...), custom_call_target="tpu_custom_call" | custom-call | flops 301989888 | bytes 3145728 | tf_op jit(solution)/shard_map/pallas_call | solution.py:84
  74.1 8.4 %collective-permute-done.17 = bf16[128,512]{1,0:T(8,128)(2,1)S(1)} collective-permute-done((bf16[128,512]{1,0:T(8,128)(2,1)S(1)}, bf16[128,512]{1,0:T(8,128)(2,1)S(1)}, u32[]{:S(2)}, u32[]{:S(2)}) %collective-permute-start.17) | collective-permute-done | bytes 131104 | tf_op jit(solution)/shard_map/ppermute | solution.py:127
  82.5 0.3 fusion.58
  82.8 0.2 fusion.3
  83.1 0.3 convolution_convert_fusion
  83.4 0.3 fusion.57
  83.7 0.2 fusion.2
  84.0 0.3 convolution_convert_fusion.1
  84.4 4.2 %collective-permute-done.18 = bf16[128,256]{0,1:T(8,128)(2,1)S(1)} collective-permute-done((bf16[128,256]{0,1:T(8,128)(2,1)S(1)}, bf16[128,256]{0,1:T(8,128)(2,1)S(1)}, u32[]{:S(2)}, u32[]{:S(2)}) %collective-permute-start.18) | collective-permute-done | bytes 65568 | tf_op jit(solution)/shard_map/ppermute | solution.py:127
  88.6 1.5 %fusion.1 = bf16[1,128,3072]{2,1,0:T(8,128)(2,1)} fusion(bf16[512,3072]{1,0:T(8,128)(2,1)S(1)} %bitcast.32, f32[3072]{0:T(1024)S(1)} %bitcast.39, bf16[128,256]{0,1:T(8,128)(2,1)S(1)} %collective-permute-done.18, bf16[128,256]{0,1:T(8,128)(2,1)S(1)} %get-tuple-element.43), kind=kOutput, calls=%fused_computation.2 | convolution fusion | flops 403701760 | bytes 4075520 | tf_op jit(solution)/shard_map/dot_general | solution.py:223
  (59 shorter events, 0.9 us)
Async XLA Ops:
  0.0 13.0 %copy-start.1 = (bf16[1,128,3072]{2,1,0:T(8,128)(2,1)S(1)}, bf16[1,128,3072]{2,1,0:T(8,128)(2,1)}, u32[]{:S(2)}) copy-start(bf16[1,128,3072]{2,1,0:T(8,128)(2,1)} %param.5) | copy-start | bytes 2359300
  0.0 29.4 %collective-permute-start = (bf16[384,384]{1,0:T(8,128)(2,1)}, bf16[384,384]{1,0:T(8,128)(2,1)S(1)}, u32[]{:S(2)}, u32[]{:S(2)}) collective-permute-start(bf16[384,384]{1,0:T(8,128)(2,1)} %bitcast.23), channel_id=1, source_target_pairs={{0,8},{1,9},{2,10},{3,11},{4,12},{5,13},{6,14},{7,15},{8,0},{9,1},... | collective-permute-start | bytes 884744 | tf_op jit(solution)/shard_map/ppermute | solution.py:127
  3.0 28.9 %collective-permute-start.1 = (bf16[384,384]{1,0:T(8,128)(2,1)}, bf16[384,384]{1,0:T(8,128)(2,1)S(1)}, u32[]{:S(2)}, u32[]{:S(2)}) collective-permute-start(bf16[384,384]{1,0:T(8,128)(2,1)} %bitcast.24), channel_id=1, source_target_pairs={{0,16},{1,17},{2,18},{3,19},{4,20},{5,21},{6,22},{7,23},{8,24},{9,... | collective-permute-start | bytes 884744 | tf_op jit(solution)/shard_map/ppermute | solution.py:127
  4.5 9.7 %collective-permute-start.19 = (bf16[16,3072]{1,0:T(8,128)(2,1)}, bf16[16,3072]{1,0:T(8,128)(2,1)S(1)}, u32[]{:S(2)}, u32[]{:S(2)}) collective-permute-start(bf16[16,3072]{1,0:T(8,128)(2,1)} %bitcast.33), channel_id=1, source_target_pairs={{0,2},{1,3},{2,0},{3,1},{4,6},{5,7},{6,4},{7,5},{8,10},{9,11},{10,... | collective-permute-start | bytes 294920 | tf_op jit(solution)/shard_map/ppermute | solution.py:127
  7.1 8.8 %collective-permute-start.20 = (bf16[16,3072]{1,0:T(8,128)(2,1)}, bf16[16,3072]{1,0:T(8,128)(2,1)S(1)}, u32[]{:S(2)}, u32[]{:S(2)}) collective-permute-start(bf16[16,3072]{1,0:T(8,128)(2,1)} %bitcast.34), channel_id=1, source_target_pairs={{0,1},{1,0},{2,3},{3,2},{4,5},{5,4},{6,7},{7,6},{8,9},{9,8},{10,11... | collective-permute-start | bytes 294920 | tf_op jit(solution)/shard_map/ppermute | solution.py:127
  8.7 7.3 %collective-permute-start.21 = (bf16[16,3072]{1,0:T(8,128)(2,1)}, bf16[16,3072]{1,0:T(8,128)(2,1)S(1)}, u32[]{:S(2)}, u32[]{:S(2)}) collective-permute-start(bf16[16,3072]{1,0:T(8,128)(2,1)} %bitcast.35), channel_id=1, source_target_pairs={{0,3},{1,2},{2,1},{3,0},{4,7},{5,6},{6,5},{7,4},{8,11},{9,10},{10,... | collective-permute-start | bytes 294920 | tf_op jit(solution)/shard_map/ppermute | solution.py:127
  9.6 4.5 %copy-start = (bf16[1,384,384]{2,1,0:T(8,128)(2,1)S(1)}, bf16[1,384,384]{2,1,0:T(8,128)(2,1)}, u32[]{:S(2)}) copy-start(bf16[1,384,384]{2,1,0:T(8,128)(2,1)} %param.8) | copy-start | bytes 884740
  9.6 6.3 %copy-start.2 = (bf16[1,16,3072]{2,1,0:T(8,128)(2,1)S(1)}, bf16[1,16,3072]{2,1,0:T(8,128)(2,1)}, u32[]{:S(2)}) copy-start(bf16[1,16,3072]{2,1,0:T(8,128)(2,1)} %param.9) | copy-start | bytes 294916
  14.2 14.7 %collective-permute-start.8 = (bf16[384,384]{1,0:T(8,128)(2,1)S(1)}, bf16[384,384]{1,0:T(8,128)(2,1)S(1)}, u32[]{:S(2)}, u32[]{:S(2)}) collective-permute-start(bf16[384,384]{1,0:T(8,128)(2,1)S(1)} %bitcast.25), channel_id=1, source_target_pairs={{0,2},{1,3},{2,0},{3,1},{4,6},{5,7},{6,4},{7,5},{8,10},{9,11},{10,... | collective-permute-start | bytes 884744 | tf_op jit(solution)/shard_map/ppermute | solution.py:127
  16.0 15.9 %collective-permute-start.22 = (bf16[4,16,3072]{2,1,0:T(8,128)(2,1)S(1)}, bf16[4,16,3072]{2,1,0:T(8,128)(2,1)S(1)}, u32[]{:S(2)}, u32[]{:S(2)}) collective-permute-start(bf16[4,16,3072]{2,1,0:T(8,128)(2,1)S(1)} %pad_maximum_fusion), channel_id=1, source_target_pairs={{0,8},{1,9},{2,10},{3,11},{4,12},{5,13},{6,14},{7,15},{8,0},{9,1},... | collective-permute-start | bytes 1179656 | tf_op jit(solution)/shard_map/ppermute | solution.py:127
  16.6 15.7 %collective-permute-start.23 = (bf16[4,16,3072]{2,1,0:T(8,128)(2,1)S(1)}, bf16[4,16,3072]{2,1,0:T(8,128)(2,1)S(1)}, u32[]{:S(2)}, u32[]{:S(2)}) collective-permute-start(bf16[4,16,3072]{2,1,0:T(8,128)(2,1)S(1)} %pad_maximum_fusion), channel_id=1, source_target_pairs={{0,16},{1,17},{2,18},{3,19},{4,20},{5,21},{6,22},{7,23},{8,24},{9,... | collective-permute-start | bytes 1179656 | tf_op jit(solution)/shard_map/ppermute | solution.py:127
  28.9 12.9 %collective-permute-start.24 = (bf16[4,16,3072]{2,1,0:T(8,128)(2,1)S(1)}, bf16[4,16,3072]{2,1,0:T(8,128)(2,1)S(1)}, u32[]{:S(2)}, u32[]{:S(2)}) collective-permute-start(bf16[4,16,3072]{2,1,0:T(8,128)(2,1)S(1)} %pad_maximum_fusion), channel_id=1, source_target_pairs={{0,24},{1,25},{2,26},{3,27},{4,28},{5,29},{6,30},{7,31},{8,16},{9,... | collective-permute-start | bytes 1179656 | tf_op jit(solution)/shard_map/ppermute | solution.py:127
  29.4 16.8 %collective-permute-start.2 = (bf16[384,384]{1,0:T(8,128)(2,1)S(1)}, bf16[384,384]{1,0:T(8,128)(2,1)S(1)}, u32[]{:S(2)}, u32[]{:S(2)}) collective-permute-start(bf16[384,384]{1,0:T(8,128)(2,1)S(1)} %bitcast.26), channel_id=1, source_target_pairs={{0,24},{1,25},{2,26},{3,27},{4,28},{5,29},{6,30},{7,31},{8,16},{9,... | collective-permute-start | bytes 884744 | tf_op jit(solution)/shard_map/ppermute | solution.py:127
  31.9 14.8 %collective-permute-start.3 = (bf16[384,384]{1,0:T(8,128)(2,1)S(1)}, bf16[384,384]{1,0:T(8,128)(2,1)S(1)}, u32[]{:S(2)}, u32[]{:S(2)}) collective-permute-start(bf16[384,384]{1,0:T(8,128)(2,1)S(1)} %bitcast.27), channel_id=1, source_target_pairs={{0,4},{1,5},{2,6},{3,7},{4,0},{5,1},{6,2},{7,3},{8,12},{9,13},{10,... | collective-permute-start | bytes 884744 | tf_op jit(solution)/shard_map/ppermute | solution.py:127
  31.9 33.3 %collective-permute-start.7 = (bf16[128,3072]{1,0:T(8,128)(2,1)S(1)}, bf16[128,3072]{1,0:T(8,128)(2,1)S(1)}, u32[]{:S(2)}, u32[]{:S(2)}) collective-permute-start(bf16[128,3072]{1,0:T(8,128)(2,1)S(1)} %bitcast.31), channel_id=1, source_target_pairs={{0,1},{1,0},{2,3},{3,2},{4,5},{5,4},{6,7},{7,6},{8,9},{9,8},{10,11... | collective-permute-start | bytes 2359304 | tf_op jit(solution)/shard_map/ppermute | solution.py:127
  32.3 15.9 %collective-permute-start.4 = (bf16[384,384]{1,0:T(8,128)(2,1)S(1)}, bf16[384,384]{1,0:T(8,128)(2,1)S(1)}, u32[]{:S(2)}, u32[]{:S(2)}) collective-permute-start(bf16[384,384]{1,0:T(8,128)(2,1)S(1)} %collective-permute-done.refs_2_), channel_id=1, source_target_pairs={{0,4},{1,5},{2,6},{3,7},{4,0},{5,1},{6,2},{7,3},{8,12},{9,13},{10,... | collective-permute-start | bytes 884744 | tf_op jit(solution)/shard_map/ppermute | solution.py:127
  41.7 8.0 %collective-permute-start.5 = (bf16[384,384]{1,0:T(8,128)(2,1)S(1)}, bf16[384,384]{1,0:T(8,128)(2,1)S(1)}, u32[]{:S(2)}, u32[]{:S(2)}) collective-permute-start(bf16[384,384]{1,0:T(8,128)(2,1)S(1)} %collective-permute-done.1.refs_3_), channel_id=1, source_target_pairs={{0,4},{1,5},{2,6},{3,7},{4,0},{5,1},{6,2},{7,3},{8,12},{9,13},{10,... | collective-permute-start | bytes 884744 | tf_op jit(solution)/shard_map/ppermute | solution.py:127
  46.2 13.5 %collective-permute-start.10 = (bf16[384,384]{1,0:T(8,128)(2,1)S(1)}, bf16[384,384]{1,0:T(8,128)(2,1)S(1)}, u32[]{:S(2)}, u32[]{:S(2)}) collective-permute-start(bf16[384,384]{1,0:T(8,128)(2,1)S(1)} %collective-permute-done.8.refs_1_), channel_id=1, source_target_pairs={{0,16},{1,17},{2,18},{3,19},{4,20},{5,21},{6,22},{7,23},{8,24},{9,... | collective-permute-start | bytes 884744 | tf_op jit(solution)/shard_map/ppermute | solution.py:127
  46.7 13.0 %collective-permute-start.11 = (bf16[384,384]{1,0:T(8,128)(2,1)S(1)}, bf16[384,384]{1,0:T(8,128)(2,1)S(1)}, u32[]{:S(2)}, u32[]{:S(2)}) collective-permute-start(bf16[384,384]{1,0:T(8,128)(2,1)S(1)} %collective-permute-done.8.refs_1_), channel_id=1, source_target_pairs={{0,24},{1,25},{2,26},{3,27},{4,28},{5,29},{6,30},{7,31},{8,16},{9,... | collective-permute-start | bytes 884744 | tf_op jit(solution)/shard_map/ppermute | solution.py:127
  48.2 12.7 %collective-permute-start.9 = (bf16[384,384]{1,0:T(8,128)(2,1)S(1)}, bf16[384,384]{1,0:T(8,128)(2,1)S(1)}, u32[]{:S(2)}, u32[]{:S(2)}) collective-permute-start(bf16[384,384]{1,0:T(8,128)(2,1)S(1)} %collective-permute-done.8.refs_1_), channel_id=1, source_target_pairs={{0,8},{1,9},{2,10},{3,11},{4,12},{5,13},{6,14},{7,15},{8,0},{9,1},... | collective-permute-start | bytes 884744 | tf_op jit(solution)/shard_map/ppermute | solution.py:127
  49.7 1.6 %collective-permute-start.6 = (bf16[384,384]{1,0:T(8,128)(2,1)S(1)}, bf16[384,384]{1,0:T(8,128)(2,1)S(1)}, u32[]{:S(2)}, u32[]{:S(2)}) collective-permute-start(bf16[384,384]{1,0:T(8,128)(2,1)S(1)} %collective-permute-done.2.refs_4_), channel_id=1, source_target_pairs={{0,4},{1,5},{2,6},{3,7},{4,0},{5,1},{6,2},{7,3},{8,12},{9,13},{10,... | collective-permute-start | bytes 884744 | tf_op jit(solution)/shard_map/ppermute | solution.py:127
  60.9 1.6 %collective-permute-start.12 = (bf16[384,384]{1,0:T(8,128)(2,1)S(1)}, bf16[384,384]{1,0:T(8,128)(2,1)S(1)}, u32[]{:S(2)}, u32[]{:S(2)}) collective-permute-start(bf16[384,384]{1,0:T(8,128)(2,1)S(1)} %collective-permute-done.8.refs_1_), channel_id=1, source_target_pairs={{0,4},{1,5},{2,6},{3,7},{4,0},{5,1},{6,2},{7,3},{8,12},{9,13},{10,... | collective-permute-start | bytes 884744 | tf_op jit(solution)/shard_map/ppermute | solution.py:127
  60.9 2.0 %collective-permute-start.13 = (bf16[384,384]{1,0:T(8,128)(2,1)S(1)}, bf16[384,384]{1,0:T(8,128)(2,1)S(1)}, u32[]{:S(2)}, u32[]{:S(2)}) collective-permute-start(bf16[384,384]{1,0:T(8,128)(2,1)S(1)} %collective-permute-done.9.refs_2_), channel_id=1, source_target_pairs={{0,4},{1,5},{2,6},{3,7},{4,0},{5,1},{6,2},{7,3},{8,12},{9,13},{10,... | collective-permute-start | bytes 884744 | tf_op jit(solution)/shard_map/ppermute | solution.py:127
  61.4 1.9 %collective-permute-start.14 = (bf16[384,384]{1,0:T(8,128)(2,1)S(1)}, bf16[384,384]{1,0:T(8,128)(2,1)S(1)}, u32[]{:S(2)}, u32[]{:S(2)}) collective-permute-start(bf16[384,384]{1,0:T(8,128)(2,1)S(1)} %collective-permute-done.10.refs_3_), channel_id=1, source_target_pairs={{0,4},{1,5},{2,6},{3,7},{4,0},{5,1},{6,2},{7,3},{8,12},{9,13},{10,... | collective-permute-start | bytes 884744 | tf_op jit(solution)/shard_map/ppermute | solution.py:127
  61.5 2.3 %collective-permute-start.15 = (bf16[384,384]{1,0:T(8,128)(2,1)S(1)}, bf16[384,384]{1,0:T(8,128)(2,1)S(1)}, u32[]{:S(2)}, u32[]{:S(2)}) collective-permute-start(bf16[384,384]{1,0:T(8,128)(2,1)S(1)} %collective-permute-done.11.refs_4_), channel_id=1, source_target_pairs={{0,4},{1,5},{2,6},{3,7},{4,0},{5,1},{6,2},{7,3},{8,12},{9,13},{10,... | collective-permute-start | bytes 884744 | tf_op jit(solution)/shard_map/ppermute | solution.py:127
  62.5 11.3 %collective-permute-start.25 = (bf16[4,16,3072]{2,1,0:T(8,128)(2,1)S(1)}, bf16[4,16,3072]{2,1,0:T(8,128)(2,1)S(1)}, u32[]{:S(2)}, u32[]{:S(2)}) collective-permute-start(bf16[4,16,3072]{2,1,0:T(8,128)(2,1)S(1)} %pad_maximum_fusion), channel_id=1, source_target_pairs={{0,4},{1,5},{2,6},{3,7},{4,0},{5,1},{6,2},{7,3},{8,12},{9,13},{10,... | collective-permute-start | bytes 1179656 | tf_op jit(solution)/shard_map/ppermute | solution.py:127
  62.9 11.0 %collective-permute-start.26 = (bf16[4,16,3072]{2,1,0:T(8,128)(2,1)S(1)}, bf16[4,16,3072]{2,1,0:T(8,128)(2,1)S(1)}, u32[]{:S(2)}, u32[]{:S(2)}) collective-permute-start(bf16[4,16,3072]{2,1,0:T(8,128)(2,1)S(1)} %collective-permute-done.22), channel_id=1, source_target_pairs={{0,4},{1,5},{2,6},{3,7},{4,0},{5,1},{6,2},{7,3},{8,12},{9,13},{10,... | collective-permute-start | bytes 1179656 | tf_op jit(solution)/shard_map/ppermute | solution.py:127
  63.4 10.6 %collective-permute-start.27 = (bf16[4,16,3072]{2,1,0:T(8,128)(2,1)S(1)}, bf16[4,16,3072]{2,1,0:T(8,128)(2,1)S(1)}, u32[]{:S(2)}, u32[]{:S(2)}) collective-permute-start(bf16[4,16,3072]{2,1,0:T(8,128)(2,1)S(1)} %collective-permute-done.23), channel_id=1, source_target_pairs={{0,4},{1,5},{2,6},{3,7},{4,0},{5,1},{6,2},{7,3},{8,12},{9,13},{10,... | collective-permute-start | bytes 1179656 | tf_op jit(solution)/shard_map/ppermute | solution.py:127
  63.8 20.6 %collective-permute-start.28 = (bf16[4,16,3072]{2,1,0:T(8,128)(2,1)S(1)}, bf16[4,16,3072]{2,1,0:T(8,128)(2,1)S(1)}, u32[]{:S(2)}, u32[]{:S(2)}) collective-permute-start(bf16[4,16,3072]{2,1,0:T(8,128)(2,1)S(1)} %collective-permute-done.24), channel_id=1, source_target_pairs={{0,4},{1,5},{2,6},{3,7},{4,0},{5,1},{6,2},{7,3},{8,12},{9,13},{10,... | collective-permute-start | bytes 1179656 | tf_op jit(solution)/shard_map/ppermute | solution.py:127
  65.3 17.2 %collective-permute-start.16 = (bf16[128,512]{1,0:T(8,128)(2,1)S(1)}, bf16[128,512]{1,0:T(8,128)(2,1)S(1)}, u32[]{:S(2)}, u32[]{:S(2)}) collective-permute-start(bf16[128,512]{1,0:T(8,128)(2,1)S(1)} %constant_dynamic-update-slice_fusion), channel_id=1, source_target_pairs={{0,2},{1,3},{2,0},{3,1},{4,6},{5,7},{6,4},{7,5},{8,10},{9,11},{10,... | collective-permute-start | bytes 393224 | tf_op jit(solution)/shard_map/ppermute | solution.py:127
  73.8 8.6 %collective-permute-start.17 = (bf16[128,512]{1,0:T(8,128)(2,1)S(1)}, bf16[128,512]{1,0:T(8,128)(2,1)S(1)}, u32[]{:S(2)}, u32[]{:S(2)}) collective-permute-start(bf16[128,512]{1,0:T(8,128)(2,1)S(1)} %pad_maximum_fusion.2), channel_id=1, source_target_pairs={{0,2},{1,3},{2,0},{3,1},{4,6},{5,7},{6,4},{7,5},{8,10},{9,11},{10,... | collective-permute-start | bytes 393224 | tf_op jit(solution)/shard_map/ppermute | solution.py:127
  84.3 4.3 %collective-permute-start.18 = (bf16[128,256]{0,1:T(8,128)(2,1)S(1)}, bf16[128,256]{0,1:T(8,128)(2,1)S(1)}, u32[]{:S(2)}, u32[]{:S(2)}) collective-permute-start(bf16[128,256]{0,1:T(8,128)(2,1)S(1)} %get-tuple-element.44), channel_id=1, source_target_pairs={{0,1},{1,0},{2,3},{3,2},{4,5},{5,4},{6,7},{7,6},{8,9},{9,8},{10,11... | collective-permute-start | bytes 196616 | tf_op jit(solution)/shard_map/ppermute | solution.py:127
where the time goes:
time: 90.3 us; the launch traced here: 90.1 us
  waiting for transfers between devices  49.3 us (55%)
  starting transfers between devices  25.3 us (28%)
  Pallas kernels  7.42 us (8%)
  matrix products  5.87 us (7%)
  between operations  0.99 us (1%)
    ppermute x29, waiting for transfers between devices, move(): return lax.ppermute(value, AXES, pairs)  49.3 us
    ppermute x29, starting transfers between devices, move(): return lax.ppermute(value, AXES, pairs)  25.3 us
    pallas_call x4, Pallas kernels, project(): pl.pallas_call(functools.partial(project_kernel, len(xs)), out_shape=(jax...  5.15 us
    dot_general x1, matrix products, modulation(): return jnp.dot(embed, w_mod, preferred_element_type=jnp.float32)  3.1 us
    pallas_call x2, Pallas kernels, normalize(): pl.pallas_call(functools.partial(normalize_kernel, block), out_shape=jax....  2.27 us
  transfers between devices with their start and end apart: 29, of which 12 were waited for; matrix products, arithmetic and copies ran while one was open for 6% of the time, Pallas kernels for 8%

commit v1 on v0

--- a/solution.py
+++ b/solution.py
@@ -178,37 +178,23 @@
     other_in = over_chips(after(other_shard, mine_normed))
     own_pieces = over_cores(own_in)
     out_mine = over_chips(after(jnp.stack(out_shards), mine_normed))
-    query_own, kv_own = project([mine_normed], own_pieces, owners, reorder)
-    other_pieces = over_cores(after(other_in, kv_own))
-
-    queries, local_kv, remote_kv = [[], []], [], []
-    for stage in range(2):
-        if stage:
-            raw = after(raw, local_kv[0])
-            xs = [normalize(rows, shift, scale) for rows in raw]
-            query_own, kv_own = project(xs, own_pieces, owners, reorder)
-        else:
-            xs = [mine_normed]
-        query_other, kv_other = project(xs, other_pieces, owners, reorder)
-        queries[0].append(query_own)
-        queries[1].append(query_other)
-        local_kv.append(jnp.concatenate([kv_own, kv_other], axis=1))
-        remote_kv.append(move(local_kv[-1], same, sp_shift(1, 0)))
+    query_mine, kv_mine = project([mine_normed], own_pieces, owners, reorder)
+    remote_mine = move(kv_mine, same, sp_shift(1, 0))
+    rest = [normalize(rows, shift, scale) for rows in after(raw, kv_mine)]
+    query_rest, kv_rest = project(rest, own_pieces, owners, reorder)
+    remote_rest = move(kv_rest, same, sp_shift(1, 0))
+    other_pieces = over_cores(after(other_in, kv_rest))
+    query_other, kv_other = project([mine_normed] + rest, other_pieces, owners, reorder)
+    remote_other = move(kv_other, same, sp_shift(1, 0))
+
+    query_both = jnp.concatenate([query_mine, query_rest], axis=0)
     heads = []
-    for index in range(2):
-        here = index * 2 * head_size
-        there = (1 - index) * 2 * head_size
-        keys = [kv[:, here : here + head_size] for kv in local_kv]
-        keys += [kv[:, there : there + head_size] for kv in remote_kv]
-        values = [kv[:, here + head_size : here + 2 * head_size] for kv in local_kv]
-        values += [kv[:, there + head_size : there + 2 * head_size] for kv in remote_kv]
-        heads.append(
-            attend(
-                jnp.concatenate(queries[index], axis=0),
-                jnp.concatenate(keys, axis=0),
-                jnp.concatenate(values, axis=0),
-            )
-        )
+    for query, parts in (
+        (query_both, [kv_mine, kv_rest, remote_other]),
+        (query_other, [kv_other, remote_mine, remote_rest]),
+    ):
+        kv = jnp.concatenate(parts, axis=0)
+        heads.append(attend(query, kv[:, :head_size], kv[:, head_size:]))
     both = jnp.concatenate(heads, axis=1)
 
     mine = []

time: 90.3 us -> 80.7 us (0.89)
  waiting for transfers between devices: 49.3 us -> 38.7 us
  starting transfers between devices: 25.3 us -> 27.1 us
    ppermute x29 -> x30, waiting for transfers between devices: 49.3 us -> 38.7 us  [move(): return lax.ppermute(value, AXES, pairs)]
    ppermute x29 -> x30, starting transfers between devices: 25.3 us -> 27.1 us  [move(): return lax.ppermute(value, AXES, pairs)]
    pallas_call x4 -> x3, Pallas kernels: 5.15 us -> 4.53 us  [project(): pl.pallas_call(functools.partial(project_kernel, len(xs)), out_shape=(jax...]
  transfers between devices with their start and end apart: 29 -> 30, of which waited for: 12 -> 10; matrix products, arithmetic and copies ran while one was open for 6% -> 7% of each run, Pallas kernels for 8% -> 8%
where the time goes in v1:
time: 80.7 us; the launch traced here: 80.6 us
  waiting for transfers between devices  38.7 us (48%)
  starting transfers between devices  27.1 us (34%)
  Pallas kernels  6.8 us (8%)
  matrix products  5.87 us (7%)
  between operations  0.95 us (1%)
    ppermute x30, waiting for transfers between devices, move(): return lax.ppermute(value, AXES, pairs)  38.7 us
    ppermute x30, starting transfers between devices, move(): return lax.ppermute(value, AXES, pairs)  27.1 us
    pallas_call x3, Pallas kernels, project(): pl.pallas_call(functools.partial(project_kernel, len(xs)), out_shape=(jax...  4.53 us
    dot_general x1, matrix products, modulation(): return jnp.dot(embed, w_mod, preferred_element_type=jnp.float32)  3.1 us
    pallas_call x2, Pallas kernels, normalize(): pl.pallas_call(functools.partial(normalize_kernel, block), out_shape=jax....  2.27 us
  transfers between devices with their start and end apart: 30, of which 10 were waited for; matrix products, arithmetic and copies ran while one was open for 7% of the time, Pallas kernels for 8%

profile of v1, /device:TPU:0, one launch (start us, length us, event | category | flops | bytes accessed | tf_op | source)
XLA Modules:
  0.0 80.6 jit_solution(17295086699133730499)
XLA Ops:
  0.0 3.0 %collective-permute-start = (bf16[384,384]{1,0:T(8,128)(2,1)}, bf16[384,384]{1,0:T(8,128)(2,1)S(1)}, u32[]{:S(2)}, u32[]{:S(2)}) collective-permute-start(bf16[384,384]{1,0:T(8,128)(2,1)} %bitcast.24), channel_id=1, source_target_pairs={{0,8},{1,9},{2,10},{3,11},{4,12},{5,13},{6,14},{7,15},{8,0},{9,1},... | collective-permute-start | bytes 884744 | tf_op jit(solution)/shard_map/ppermute | solution.py:127
  3.0 1.5 %collective-permute-start.1 = (bf16[384,384]{1,0:T(8,128)(2,1)}, bf16[384,384]{1,0:T(8,128)(2,1)S(1)}, u32[]{:S(2)}, u32[]{:S(2)}) collective-permute-start(bf16[384,384]{1,0:T(8,128)(2,1)} %bitcast.25), channel_id=1, source_target_pairs={{0,16},{1,17},{2,18},{3,19},{4,20},{5,21},{6,22},{7,23},{8,24},{9,... | collective-permute-start | bytes 884744 | tf_op jit(solution)/shard_map/ppermute | solution.py:127
  4.5 2.6 %collective-permute-start.20 = (bf16[16,3072]{1,0:T(8,128)(2,1)}, bf16[16,3072]{1,0:T(8,128)(2,1)S(1)}, u32[]{:S(2)}, u32[]{:S(2)}) collective-permute-start(bf16[16,3072]{1,0:T(8,128)(2,1)} %bitcast.34), channel_id=1, source_target_pairs={{0,2},{1,3},{2,0},{3,1},{4,6},{5,7},{6,4},{7,5},{8,10},{9,11},{10,... | collective-permute-start | bytes 294920 | tf_op jit(solution)/shard_map/ppermute | solution.py:127
  7.1 1.6 %collective-permute-start.21 = (bf16[16,3072]{1,0:T(8,128)(2,1)}, bf16[16,3072]{1,0:T(8,128)(2,1)S(1)}, u32[]{:S(2)}, u32[]{:S(2)}) collective-permute-start(bf16[16,3072]{1,0:T(8,128)(2,1)} %bitcast.35), channel_id=1, source_target_pairs={{0,1},{1,0},{2,3},{3,2},{4,5},{5,4},{6,7},{7,6},{8,9},{9,8},{10,11... | collective-permute-start | bytes 294920 | tf_op jit(solution)/shard_map/ppermute | solution.py:127
  8.7 0.2 collective-permute-start.22
  9.6 3.1 %fusion.23 = f32[1,9216]{1,0:T(1,128)S(1)} fusion(bf16[256,1]{0,1:T(2,128)(2,1)S(1)} %reshape.45, bf16[256,9216]{1,0:T(8,128)(2,1)} %param.7), kind=kOutput, calls=%fused_computation.59 | convolution fusion | flops 4718592 | bytes 4755968 | tf_op jit(solution)/shard_map/dot_general | solution.py:20
  12.7 0.1 stack.47.owner_ref
  12.8 0.1 broadcast_in_dim.4
  12.9 0.1 mul.74
  13.0 1.1 %shard_map.55.refs_0_ = bf16[128,3072]{1,0:T(8,128)(2,1)S(1)} custom-call(bf16[128,3072]{1,0:T(8,128)(2,1)S(1)} %bitcast.31, f32[1,3072]{1,0:T(1,128)S(1)} %get-tuple-element.42.shift_ref, f32[1,3072]{1,0:T(1,128)S(1)} %get-tuple-element.43.scale_ref), custom_call_target="tpu_custom_call" | custom-call | flops 3932160 | bytes 1572864 | tf_op jit(solution)/shard_map/pallas_call | solution.py:39
  14.2 0.3 collective-permute-start.2
  14.5 1.9 %collective-permute-start.8 = (bf16[384,384]{1,0:T(8,128)(2,1)S(1)}, bf16[384,384]{1,0:T(8,128)(2,1)S(1)}, u32[]{:S(2)}, u32[]{:S(2)}) collective-permute-start(bf16[384,384]{1,0:T(8,128)(2,1)S(1)} %bitcast.27), channel_id=1, source_target_pairs={{0,2},{1,3},{2,0},{3,1},{4,6},{5,7},{6,4},{7,5},{8,10},{9,11},{10,... | collective-permute-start | bytes 884744 | tf_op jit(solution)/shard_map/ppermute | solution.py:127
  16.5 1.6 %collective-permute-start.23 = (bf16[4,16,3072]{2,1,0:T(8,128)(2,1)S(1)}, bf16[4,16,3072]{2,1,0:T(8,128)(2,1)S(1)}, u32[]{:S(2)}, u32[]{:S(2)}) collective-permute-start(bf16[4,16,3072]{2,1,0:T(8,128)(2,1)S(1)} %pad_maximum_fusion), channel_id=1, source_target_pairs={{0,8},{1,9},{2,10},{3,11},{4,12},{5,13},{6,14},{7,15},{8,0},{9,1},... | collective-permute-start | bytes 1179656 | tf_op jit(solution)/shard_map/ppermute | solution.py:127
  18.0 1.5 %collective-permute-start.24 = (bf16[4,16,3072]{2,1,0:T(8,128)(2,1)S(1)}, bf16[4,16,3072]{2,1,0:T(8,128)(2,1)S(1)}, u32[]{:S(2)}, u32[]{:S(2)}) collective-permute-start(bf16[4,16,3072]{2,1,0:T(8,128)(2,1)S(1)} %pad_maximum_fusion), channel_id=1, source_target_pairs={{0,16},{1,17},{2,18},{3,19},{4,20},{5,21},{6,22},{7,23},{8,24},{9,... | collective-permute-start | bytes 1179656 | tf_op jit(solution)/shard_map/ppermute | solution.py:127
  19.6 9.5 %collective-permute-done.8.refs_2_ = bf16[384,384]{1,0:T(8,128)(2,1)S(1)} collective-permute-done((bf16[384,384]{1,0:T(8,128)(2,1)S(1)}, bf16[384,384]{1,0:T(8,128)(2,1)S(1)}, u32[]{:S(2)}, u32[]{:S(2)}) %collective-permute-start.8) | collective-permute-done | bytes 294944 | tf_op jit(solution)/shard_map/ppermute | solution.py:127
  29.1 2.4 %collective-permute-start.25 = (bf16[4,16,3072]{2,1,0:T(8,128)(2,1)S(1)}, bf16[4,16,3072]{2,1,0:T(8,128)(2,1)S(1)}, u32[]{:S(2)}, u32[]{:S(2)}) collective-permute-start(bf16[4,16,3072]{2,1,0:T(8,128)(2,1)S(1)} %pad_maximum_fusion), channel_id=1, source_target_pairs={{0,24},{1,25},{2,26},{3,27},{4,28},{5,29},{6,30},{7,31},{8,16},{9,... | collective-permute-start | bytes 1179656 | tf_op jit(solution)/shard_map/ppermute | solution.py:127
  31.7 0.5 collective-permute-start.4
  32.2 0.1 collective-permute-start.5
  32.3 7.8 %collective-permute-done.25 = bf16[4,16,3072]{2,1,0:T(8,128)(2,1)S(1)} collective-permute-done((bf16[4,16,3072]{2,1,0:T(8,128)(2,1)S(1)}, bf16[4,16,3072]{2,1,0:T(8,128)(2,1)S(1)}, u32[]{:S(2)}, u32[]{:S(2)}) %collective-permute-start.25) | collective-permute-done | bytes 393248 | tf_op jit(solution)/shard_map/ppermute | solution.py:127
  40.2 1.6 %collective-permute-start.10 = (bf16[384,384]{1,0:T(8,128)(2,1)S(1)}, bf16[384,384]{1,0:T(8,128)(2,1)S(1)}, u32[]{:S(2)}, u32[]{:S(2)}) collective-permute-start(bf16[384,384]{1,0:T(8,128)(2,1)S(1)} %collective-permute-done.8.refs_2_), channel_id=1, source_target_pairs={{0,16},{1,17},{2,18},{3,19},{4,20},{5,21},{6,22},{7,23},{8,24},{9,... | collective-permute-start | bytes 884744 | tf_op jit(solution)/shard_map/ppermute | solution.py:127
  41.8 1.4 %collective-permute-start.11 = (bf16[384,384]{1,0:T(8,128)(2,1)S(1)}, bf16[384,384]{1,0:T(8,128)(2,1)S(1)}, u32[]{:S(2)}, u32[]{:S(2)}) collective-permute-start(bf16[384,384]{1,0:T(8,128)(2,1)S(1)} %collective-permute-done.8.refs_2_), channel_id=1, source_target_pairs={{0,24},{1,25},{2,26},{3,27},{4,28},{5,29},{6,30},{7,31},{8,16},{9,... | collective-permute-start | bytes 884744 | tf_op jit(solution)/shard_map/ppermute | solution.py:127
  43.2 0.5 collective-permute-start.9
  43.8 1.3 %shard_map.56 = (bf16[128,128]{1,0:T(8,128)(2,1)S(1)}, bf16[128,256]{1,0:T(8,128)(2,1)S(1)}) custom-call(s32[8]{0:T(128)S(1)} %stack.47.owner_ref, bf16[128,128]{1,0:T(8,128)(2,1)S(1)} %fusion.16.reorder_ref, bf16[128,3072]{1,0:T(8,128)(2,1)S(1)} %shard_map.55.refs_0_, bf16[384,384]{1,0:T(8,128)(2,1)S(1)} %bitcast.29, ...), custom_call_target="tpu_custom_call" | custom-call | flops 301989888 | bytes 3145728 | tf_op jit(solution)/shard_map/pallas_call | solution.py:84
  45.1 6.4 %collective-permute-done.7.x_ref = bf16[128,3072]{1,0:T(8,128)(2,1)S(1)} collective-permute-done((bf16[128,3072]{1,0:T(8,128)(2,1)S(1)}, bf16[128,3072]{1,0:T(8,128)(2,1)S(1)}, u32[]{:S(2)}, u32[]{:S(2)}) %collective-permute-start.7) | collective-permute-done | bytes 786464 | tf_op jit(solution)/shard_map/ppermute | solution.py:127
  51.6 1.1 %shard_map.57.refs_0_.refs_1_ = bf16[128,3072]{1,0:T(8,128)(2,1)S(1)} custom-call(bf16[128,3072]{1,0:T(8,128)(2,1)S(1)} %collective-permute-done.7.x_ref, f32[1,3072]{1,0:T(1,128)S(1)} %get-tuple-element.42.shift_ref, f32[1,3072]{1,0:T(1,128)S(1)} %get-tuple-element.43.scale_ref), custom_call_target="tpu_custom_call" | custom-call | flops 3932160 | bytes 1572864 | tf_op jit(solution)/shard_map/pallas_call | solution.py:39
  52.7 1.3 %shard_map.58 = (bf16[128,128]{1,0:T(8,128)(2,1)S(1)}, bf16[128,256]{1,0:T(8,128)(2,1)S(1)}) custom-call(s32[8]{0:T(128)S(1)} %stack.47.owner_ref, bf16[128,128]{1,0:T(8,128)(2,1)S(1)} %fusion.16.reorder_ref, bf16[128,3072]{1,0:T(8,128)(2,1)S(1)} %shard_map.57.refs_0_.refs_1_, bf16[384,384]{1,0:T(8,128)(2,1)S(1)} %bitcast.30, ...), custom_call_target="tpu_custom_call" | custom-call | flops 301989888 | bytes 3145728 | tf_op jit(solution)/shard_map/pallas_call | solution.py:84
  54.0 2.0 %collective-permute-done.10.refs_4_ = bf16[384,384]{1,0:T(8,128)(2,1)S(1)} collective-permute-done((bf16[384,384]{1,0:T(8,128)(2,1)S(1)}, bf16[384,384]{1,0:T(8,128)(2,1)S(1)}, u32[]{:S(2)}, u32[]{:S(2)}) %collective-permute-start.10) | collective-permute-done | bytes 294944 | tf_op jit(solution)/shard_map/ppermute | solution.py:127
  56.0 0.5 collective-permute-start.29
  56.5 0.7 collective-permute-done.9.refs_3_
  57.3 0.6 collective-permute-start.13
  57.9 0.1 collective-permute-start.14
  58.0 0.6 collective-permute-start.15
  58.6 0.2 collective-permute-done.12.refs_6_
  58.8 1.5 %collective-permute-start.17 = (bf16[128,256]{1,0:T(8,128)(2,1)S(1)}, bf16[128,256]{1,0:T(8,128)(2,1)S(1)}, u32[]{:S(2)}, u32[]{:S(2)}) collective-permute-start(bf16[128,256]{1,0:T(8,128)(2,1)S(1)} %get-tuple-element.23), channel_id=1, source_target_pairs={{0,2},{1,3},{2,0},{3,1},{4,6},{5,7},{6,4},{7,5},{8,10},{9,11},{10,... | collective-permute-start | bytes 196616 | tf_op jit(solution)/shard_map/ppermute | solution.py:127
  60.3 1.5 %collective-permute-start.18 = (bf16[128,256]{1,0:T(8,128)(2,1)S(1)}, bf16[128,256]{1,0:T(8,128)(2,1)S(1)}, u32[]{:S(2)}, u32[]{:S(2)}) collective-permute-start(bf16[128,256]{1,0:T(8,128)(2,1)S(1)} %get-tuple-element.26), channel_id=1, source_target_pairs={{0,2},{1,3},{2,0},{3,1},{4,6},{5,7},{6,4},{7,5},{8,10},{9,11},{10,... | collective-permute-start | bytes 196616 | tf_op jit(solution)/shard_map/ppermute | solution.py:127
  61.8 1.9 %shard_map.59 = (bf16[256,128]{1,0:T(8,128)(2,1)S(1)}, bf16[256,256]{1,0:T(8,128)(2,1)S(1)}) custom-call(s32[8]{0:T(128)S(1)} %stack.47.owner_ref, bf16[128,128]{1,0:T(8,128)(2,1)S(1)} %fusion.16.reorder_ref, bf16[128,3072]{1,0:T(8,128)(2,1)S(1)} %shard_map.55.refs_0_, bf16[128,3072]{1,0:T(8,128)(2,1)S(1)} %shard_map.57.refs_0_.refs_1_, ...), custom_call_target="tpu_custom_call" | custom-call | flops 603979776 | bytes 3932160 | tf_op jit(solution)/shard_map/pallas_call | solution.py:84
  63.7 1.5 %collective-permute-start.16 = (bf16[256,256]{1,0:T(8,128)(2,1)S(1)}, bf16[256,256]{1,0:T(8,128)(2,1)S(1)}, u32[]{:S(2)}, u32[]{:S(2)}) collective-permute-start(bf16[256,256]{1,0:T(8,128)(2,1)S(1)} %get-tuple-element.32), channel_id=1, source_target_pairs={{0,2},{1,3},{2,0},{3,1},{4,6},{5,7},{6,4},{7,5},{8,10},{9,11},{10,... | collective-permute-start | bytes 393224 | tf_op jit(solution)/shard_map/ppermute | solution.py:127
  65.3 0.6 collective-permute-done.17
  65.9 5.6 %collective-permute-done.18 = bf16[128,256]{1,0:T(8,128)(2,1)S(1)} collective-permute-done((bf16[128,256]{1,0:T(8,128)(2,1)S(1)}, bf16[128,256]{1,0:T(8,128)(2,1)S(1)}, u32[]{:S(2)}, u32[]{:S(2)}) %collective-permute-start.18) | collective-permute-done | bytes 65568 | tf_op jit(solution)/shard_map/ppermute | solution.py:127
  71.5 0.3 fusion.22
  71.8 0.2 fusion.3
  72.0 0.3 convolution_convert_fusion
  72.3 1.5 %collective-permute-done.16 = bf16[256,256]{1,0:T(8,128)(2,1)S(1)} collective-permute-done((bf16[256,256]{1,0:T(8,128)(2,1)S(1)}, bf16[256,256]{1,0:T(8,128)(2,1)S(1)}, u32[]{:S(2)}, u32[]{:S(2)}) %collective-permute-start.16) | collective-permute-done | bytes 131104 | tf_op jit(solution)/shard_map/ppermute | solution.py:127
  73.8 0.3 fusion.21
  74.2 0.2 fusion.2
  74.4 0.3 convolution_convert_fusion.1
  74.9 4.2 %collective-permute-done.19 = bf16[128,256]{0,1:T(8,128)(2,1)S(1)} collective-permute-done((bf16[128,256]{0,1:T(8,128)(2,1)S(1)}, bf16[128,256]{0,1:T(8,128)(2,1)S(1)}, u32[]{:S(2)}, u32[]{:S(2)}) %collective-permute-start.19) | collective-permute-done | bytes 65568 | tf_op jit(solution)/shard_map/ppermute | solution.py:127
  79.1 1.5 %fusion.1 = bf16[1,128,3072]{2,1,0:T(8,128)(2,1)} fusion(bf16[512,3072]{1,0:T(8,128)(2,1)S(1)} %bitcast.33, f32[3072]{0:T(1024)S(1)} %bitcast.40, bf16[128,256]{0,1:T(8,128)(2,1)S(1)} %collective-permute-done.19, bf16[128,256]{0,1:T(8,128)(2,1)S(1)} %get-tuple-element.39), kind=kOutput, calls=%fused_computation.2 | convolution fusion | flops 403701760 | bytes 4075520 | tf_op jit(solution)/shard_map/dot_general | solution.py:209
  (57 shorter events, 0.7 us)
Async XLA Ops:
  0.0 13.0 %copy-start.1 = (bf16[1,128,3072]{2,1,0:T(8,128)(2,1)S(1)}, bf16[1,128,3072]{2,1,0:T(8,128)(2,1)}, u32[]{:S(2)}) copy-start(bf16[1,128,3072]{2,1,0:T(8,128)(2,1)} %param.5) | copy-start | bytes 2359300
  0.0 18.0 %collective-permute-start = (bf16[384,384]{1,0:T(8,128)(2,1)}, bf16[384,384]{1,0:T(8,128)(2,1)S(1)}, u32[]{:S(2)}, u32[]{:S(2)}) collective-permute-start(bf16[384,384]{1,0:T(8,128)(2,1)} %bitcast.24), channel_id=1, source_target_pairs={{0,8},{1,9},{2,10},{3,11},{4,12},{5,13},{6,14},{7,15},{8,0},{9,1},... | collective-permute-start | bytes 884744 | tf_op jit(solution)/shard_map/ppermute | solution.py:127
  3.0 28.6 %collective-permute-start.1 = (bf16[384,384]{1,0:T(8,128)(2,1)}, bf16[384,384]{1,0:T(8,128)(2,1)S(1)}, u32[]{:S(2)}, u32[]{:S(2)}) collective-permute-start(bf16[384,384]{1,0:T(8,128)(2,1)} %bitcast.25), channel_id=1, source_target_pairs={{0,16},{1,17},{2,18},{3,19},{4,20},{5,21},{6,22},{7,23},{8,24},{9,... | collective-permute-start | bytes 884744 | tf_op jit(solution)/shard_map/ppermute | solution.py:127
  4.5 9.7 %collective-permute-start.20 = (bf16[16,3072]{1,0:T(8,128)(2,1)}, bf16[16,3072]{1,0:T(8,128)(2,1)S(1)}, u32[]{:S(2)}, u32[]{:S(2)}) collective-permute-start(bf16[16,3072]{1,0:T(8,128)(2,1)} %bitcast.34), channel_id=1, source_target_pairs={{0,2},{1,3},{2,0},{3,1},{4,6},{5,7},{6,4},{7,5},{8,10},{9,11},{10,... | collective-permute-start | bytes 294920 | tf_op jit(solution)/shard_map/ppermute | solution.py:127
  7.1 7.4 %collective-permute-start.21 = (bf16[16,3072]{1,0:T(8,128)(2,1)}, bf16[16,3072]{1,0:T(8,128)(2,1)S(1)}, u32[]{:S(2)}, u32[]{:S(2)}) collective-permute-start(bf16[16,3072]{1,0:T(8,128)(2,1)} %bitcast.35), channel_id=1, source_target_pairs={{0,1},{1,0},{2,3},{3,2},{4,5},{5,4},{6,7},{7,6},{8,9},{9,8},{10,11... | collective-permute-start | bytes 294920 | tf_op jit(solution)/shard_map/ppermute | solution.py:127
  8.7 7.8 %collective-permute-start.22 = (bf16[16,3072]{1,0:T(8,128)(2,1)}, bf16[16,3072]{1,0:T(8,128)(2,1)S(1)}, u32[]{:S(2)}, u32[]{:S(2)}) collective-permute-start(bf16[16,3072]{1,0:T(8,128)(2,1)} %bitcast.36), channel_id=1, source_target_pairs={{0,3},{1,2},{2,1},{3,0},{4,7},{5,6},{6,5},{7,4},{8,11},{9,10},{10,... | collective-permute-start | bytes 294920 | tf_op jit(solution)/shard_map/ppermute | solution.py:127
  9.6 4.5 %copy-start = (bf16[1,384,384]{2,1,0:T(8,128)(2,1)S(1)}, bf16[1,384,384]{2,1,0:T(8,128)(2,1)}, u32[]{:S(2)}) copy-start(bf16[1,384,384]{2,1,0:T(8,128)(2,1)} %param.8) | copy-start | bytes 884740
  9.6 6.8 %copy-start.2 = (bf16[1,16,3072]{2,1,0:T(8,128)(2,1)S(1)}, bf16[1,16,3072]{2,1,0:T(8,128)(2,1)}, u32[]{:S(2)}) copy-start(bf16[1,16,3072]{2,1,0:T(8,128)(2,1)} %param.9) | copy-start | bytes 294916
  14.2 17.5 %collective-permute-start.2 = (bf16[384,384]{1,0:T(8,128)(2,1)S(1)}, bf16[384,384]{1,0:T(8,128)(2,1)S(1)}, u32[]{:S(2)}, u32[]{:S(2)}) collective-permute-start(bf16[384,384]{1,0:T(8,128)(2,1)S(1)} %bitcast.26), channel_id=1, source_target_pairs={{0,24},{1,25},{2,26},{3,27},{4,28},{5,29},{6,30},{7,31},{8,16},{9,... | collective-permute-start | bytes 884744 | tf_op jit(solution)/shard_map/ppermute | solution.py:127
  14.5 14.6 %collective-permute-start.8 = (bf16[384,384]{1,0:T(8,128)(2,1)S(1)}, bf16[384,384]{1,0:T(8,128)(2,1)S(1)}, u32[]{:S(2)}, u32[]{:S(2)}) collective-permute-start(bf16[384,384]{1,0:T(8,128)(2,1)S(1)} %bitcast.27), channel_id=1, source_target_pairs={{0,2},{1,3},{2,0},{3,1},{4,6},{5,7},{6,4},{7,5},{8,10},{9,11},{10,... | collective-permute-start | bytes 884744 | tf_op jit(solution)/shard_map/ppermute | solution.py:127
  16.5 15.2 %collective-permute-start.23 = (bf16[4,16,3072]{2,1,0:T(8,128)(2,1)S(1)}, bf16[4,16,3072]{2,1,0:T(8,128)(2,1)S(1)}, u32[]{:S(2)}, u32[]{:S(2)}) collective-permute-start(bf16[4,16,3072]{2,1,0:T(8,128)(2,1)S(1)} %pad_maximum_fusion), channel_id=1, source_target_pairs={{0,8},{1,9},{2,10},{3,11},{4,12},{5,13},{6,14},{7,15},{8,0},{9,1},... | collective-permute-start | bytes 1179656 | tf_op jit(solution)/shard_map/ppermute | solution.py:127
  18.0 14.2 %collective-permute-start.24 = (bf16[4,16,3072]{2,1,0:T(8,128)(2,1)S(1)}, bf16[4,16,3072]{2,1,0:T(8,128)(2,1)S(1)}, u32[]{:S(2)}, u32[]{:S(2)}) collective-permute-start(bf16[4,16,3072]{2,1,0:T(8,128)(2,1)S(1)} %pad_maximum_fusion), channel_id=1, source_target_pairs={{0,16},{1,17},{2,18},{3,19},{4,20},{5,21},{6,22},{7,23},{8,24},{9,... | collective-permute-start | bytes 1179656 | tf_op jit(solution)/shard_map/ppermute | solution.py:127
  29.1 11.0 %collective-permute-start.25 = (bf16[4,16,3072]{2,1,0:T(8,128)(2,1)S(1)}, bf16[4,16,3072]{2,1,0:T(8,128)(2,1)S(1)}, u32[]{:S(2)}, u32[]{:S(2)}) collective-permute-start(bf16[4,16,3072]{2,1,0:T(8,128)(2,1)S(1)} %pad_maximum_fusion), channel_id=1, source_target_pairs={{0,24},{1,25},{2,26},{3,27},{4,28},{5,29},{6,30},{7,31},{8,16},{9,... | collective-permute-start | bytes 1179656 | tf_op jit(solution)/shard_map/ppermute | solution.py:127
  31.5 8.7 %collective-permute-start.3 = (bf16[384,384]{1,0:T(8,128)(2,1)S(1)}, bf16[384,384]{1,0:T(8,128)(2,1)S(1)}, u32[]{:S(2)}, u32[]{:S(2)}) collective-permute-start(bf16[384,384]{1,0:T(8,128)(2,1)S(1)} %bitcast.28), channel_id=1, source_target_pairs={{0,4},{1,5},{2,6},{3,7},{4,0},{5,1},{6,2},{7,3},{8,12},{9,13},{10,... | collective-permute-start | bytes 884744 | tf_op jit(solution)/shard_map/ppermute | solution.py:127
  31.6 19.9 %collective-permute-start.7 = (bf16[128,3072]{1,0:T(8,128)(2,1)S(1)}, bf16[128,3072]{1,0:T(8,128)(2,1)S(1)}, u32[]{:S(2)}, u32[]{:S(2)}) collective-permute-start(bf16[128,3072]{1,0:T(8,128)(2,1)S(1)} %bitcast.32), channel_id=1, source_target_pairs={{0,1},{1,0},{2,3},{3,2},{4,5},{5,4},{6,7},{7,6},{8,9},{9,8},{10,11... | collective-permute-start | bytes 2359304 | tf_op jit(solution)/shard_map/ppermute | solution.py:127
  31.7 10.1 %collective-permute-start.4 = (bf16[384,384]{1,0:T(8,128)(2,1)S(1)}, bf16[384,384]{1,0:T(8,128)(2,1)S(1)}, u32[]{:S(2)}, u32[]{:S(2)}) collective-permute-start(bf16[384,384]{1,0:T(8,128)(2,1)S(1)} %collective-permute-done.refs_2_), channel_id=1, source_target_pairs={{0,4},{1,5},{2,6},{3,7},{4,0},{5,1},{6,2},{7,3},{8,12},{9,13},{10,... | collective-permute-start | bytes 884744 | tf_op jit(solution)/shard_map/ppermute | solution.py:127
  32.2 11.0 %collective-permute-start.5 = (bf16[384,384]{1,0:T(8,128)(2,1)S(1)}, bf16[384,384]{1,0:T(8,128)(2,1)S(1)}, u32[]{:S(2)}, u32[]{:S(2)}) collective-permute-start(bf16[384,384]{1,0:T(8,128)(2,1)S(1)} %collective-permute-done.1.refs_3_), channel_id=1, source_target_pairs={{0,4},{1,5},{2,6},{3,7},{4,0},{5,1},{6,2},{7,3},{8,12},{9,13},{10,... | collective-permute-start | bytes 884744 | tf_op jit(solution)/shard_map/ppermute | solution.py:127
  40.1 3.7 %collective-permute-start.6 = (bf16[384,384]{1,0:T(8,128)(2,1)S(1)}, bf16[384,384]{1,0:T(8,128)(2,1)S(1)}, u32[]{:S(2)}, u32[]{:S(2)}) collective-permute-start(bf16[384,384]{1,0:T(8,128)(2,1)S(1)} %collective-permute-done.2.refs_4_), channel_id=1, source_target_pairs={{0,4},{1,5},{2,6},{3,7},{4,0},{5,1},{6,2},{7,3},{8,12},{9,13},{10,... | collective-permute-start | bytes 884744 | tf_op jit(solution)/shard_map/ppermute | solution.py:127
  40.2 15.8 %collective-permute-start.10 = (bf16[384,384]{1,0:T(8,128)(2,1)S(1)}, bf16[384,384]{1,0:T(8,128)(2,1)S(1)}, u32[]{:S(2)}, u32[]{:S(2)}) collective-permute-start(bf16[384,384]{1,0:T(8,128)(2,1)S(1)} %collective-permute-done.8.refs_2_), channel_id=1, source_target_pairs={{0,16},{1,17},{2,18},{3,19},{4,20},{5,21},{6,22},{7,23},{8,24},{9,... | collective-permute-start | bytes 884744 | tf_op jit(solution)/shard_map/ppermute | solution.py:127
  41.8 14.2 %collective-permute-start.11 = (bf16[384,384]{1,0:T(8,128)(2,1)S(1)}, bf16[384,384]{1,0:T(8,128)(2,1)S(1)}, u32[]{:S(2)}, u32[]{:S(2)}) collective-permute-start(bf16[384,384]{1,0:T(8,128)(2,1)S(1)} %collective-permute-done.8.refs_2_), channel_id=1, source_target_pairs={{0,24},{1,25},{2,26},{3,27},{4,28},{5,29},{6,30},{7,31},{8,16},{9,... | collective-permute-start | bytes 884744 | tf_op jit(solution)/shard_map/ppermute | solution.py:127
  43.2 14.0 %collective-permute-start.9 = (bf16[384,384]{1,0:T(8,128)(2,1)S(1)}, bf16[384,384]{1,0:T(8,128)(2,1)S(1)}, u32[]{:S(2)}, u32[]{:S(2)}) collective-permute-start(bf16[384,384]{1,0:T(8,128)(2,1)S(1)} %collective-permute-done.8.refs_2_), channel_id=1, source_target_pairs={{0,8},{1,9},{2,10},{3,11},{4,12},{5,13},{6,14},{7,15},{8,0},{9,1},... | collective-permute-start | bytes 884744 | tf_op jit(solution)/shard_map/ppermute | solution.py:127
  43.8 13.5 %collective-permute-start.26 = (bf16[4,16,3072]{2,1,0:T(8,128)(2,1)S(1)}, bf16[4,16,3072]{2,1,0:T(8,128)(2,1)S(1)}, u32[]{:S(2)}, u32[]{:S(2)}) collective-permute-start(bf16[4,16,3072]{2,1,0:T(8,128)(2,1)S(1)} %pad_maximum_fusion), channel_id=1, source_target_pairs={{0,4},{1,5},{2,6},{3,7},{4,0},{5,1},{6,2},{7,3},{8,12},{9,13},{10,... | collective-permute-start | bytes 1179656 | tf_op jit(solution)/shard_map/ppermute | solution.py:127
  51.6 6.3 %collective-permute-start.27 = (bf16[4,16,3072]{2,1,0:T(8,128)(2,1)S(1)}, bf16[4,16,3072]{2,1,0:T(8,128)(2,1)S(1)}, u32[]{:S(2)}, u32[]{:S(2)}) collective-permute-start(bf16[4,16,3072]{2,1,0:T(8,128)(2,1)S(1)} %collective-permute-done.23), channel_id=1, source_target_pairs={{0,4},{1,5},{2,6},{3,7},{4,0},{5,1},{6,2},{7,3},{8,12},{9,13},{10,... | collective-permute-start | bytes 1179656 | tf_op jit(solution)/shard_map/ppermute | solution.py:127
  56.0 2.0 %collective-permute-start.28 = (bf16[4,16,3072]{2,1,0:T(8,128)(2,1)S(1)}, bf16[4,16,3072]{2,1,0:T(8,128)(2,1)S(1)}, u32[]{:S(2)}, u32[]{:S(2)}) collective-permute-start(bf16[4,16,3072]{2,1,0:T(8,128)(2,1)S(1)} %collective-permute-done.24), channel_id=1, source_target_pairs={{0,4},{1,5},{2,6},{3,7},{4,0},{5,1},{6,2},{7,3},{8,12},{9,13},{10,... | collective-permute-start | bytes 1179656 | tf_op jit(solution)/shard_map/ppermute | solution.py:127
  56.0 18.8 %collective-permute-start.29 = (bf16[4,16,3072]{2,1,0:T(8,128)(2,1)S(1)}, bf16[4,16,3072]{2,1,0:T(8,128)(2,1)S(1)}, u32[]{:S(2)}, u32[]{:S(2)}) collective-permute-start(bf16[4,16,3072]{2,1,0:T(8,128)(2,1)S(1)} %collective-permute-done.25), channel_id=1, source_target_pairs={{0,4},{1,5},{2,6},{3,7},{4,0},{5,1},{6,2},{7,3},{8,12},{9,13},{10,... | collective-permute-start | bytes 1179656 | tf_op jit(solution)/shard_map/ppermute | solution.py:127
  57.3 1.6 %collective-permute-start.12 = (bf16[384,384]{1,0:T(8,128)(2,1)S(1)}, bf16[384,384]{1,0:T(8,128)(2,1)S(1)}, u32[]{:S(2)}, u32[]{:S(2)}) collective-permute-start(bf16[384,384]{1,0:T(8,128)(2,1)S(1)} %collective-permute-done.8.refs_2_), channel_id=1, source_target_pairs={{0,4},{1,5},{2,6},{3,7},{4,0},{5,1},{6,2},{7,3},{8,12},{9,13},{10,... | collective-permute-start | bytes 884744 | tf_op jit(solution)/shard_map/ppermute | solution.py:127
  57.3 3.0 %collective-permute-start.13 = (bf16[384,384]{1,0:T(8,128)(2,1)S(1)}, bf16[384,384]{1,0:T(8,128)(2,1)S(1)}, u32[]{:S(2)}, u32[]{:S(2)}) collective-permute-start(bf16[384,384]{1,0:T(8,128)(2,1)S(1)} %collective-permute-done.9.refs_3_), channel_id=1, source_target_pairs={{0,4},{1,5},{2,6},{3,7},{4,0},{5,1},{6,2},{7,3},{8,12},{9,13},{10,... | collective-permute-start | bytes 884744 | tf_op jit(solution)/shard_map/ppermute | solution.py:127
  57.9 3.9 %collective-permute-start.14 = (bf16[384,384]{1,0:T(8,128)(2,1)S(1)}, bf16[384,384]{1,0:T(8,128)(2,1)S(1)}, u32[]{:S(2)}, u32[]{:S(2)}) collective-permute-start(bf16[384,384]{1,0:T(8,128)(2,1)S(1)} %collective-permute-done.10.refs_4_), channel_id=1, source_target_pairs={{0,4},{1,5},{2,6},{3,7},{4,0},{5,1},{6,2},{7,3},{8,12},{9,13},{10,... | collective-permute-start | bytes 884744 | tf_op jit(solution)/shard_map/ppermute | solution.py:127
  58.0 3.8 %collective-permute-start.15 = (bf16[384,384]{1,0:T(8,128)(2,1)S(1)}, bf16[384,384]{1,0:T(8,128)(2,1)S(1)}, u32[]{:S(2)}, u32[]{:S(2)}) collective-permute-start(bf16[384,384]{1,0:T(8,128)(2,1)S(1)} %collective-permute-done.11.refs_5_), channel_id=1, source_target_pairs={{0,4},{1,5},{2,6},{3,7},{4,0},{5,1},{6,2},{7,3},{8,12},{9,13},{10,... | collective-permute-start | bytes 884744 | tf_op jit(solution)/shard_map/ppermute | solution.py:127
  58.8 7.0 %collective-permute-start.17 = (bf16[128,256]{1,0:T(8,128)(2,1)S(1)}, bf16[128,256]{1,0:T(8,128)(2,1)S(1)}, u32[]{:S(2)}, u32[]{:S(2)}) collective-permute-start(bf16[128,256]{1,0:T(8,128)(2,1)S(1)} %get-tuple-element.23), channel_id=1, source_target_pairs={{0,2},{1,3},{2,0},{3,1},{4,6},{5,7},{6,4},{7,5},{8,10},{9,11},{10,... | collective-permute-start | bytes 196616 | tf_op jit(solution)/shard_map/ppermute | solution.py:127
  60.3 11.2 %collective-permute-start.18 = (bf16[128,256]{1,0:T(8,128)(2,1)S(1)}, bf16[128,256]{1,0:T(8,128)(2,1)S(1)}, u32[]{:S(2)}, u32[]{:S(2)}) collective-permute-start(bf16[128,256]{1,0:T(8,128)(2,1)S(1)} %get-tuple-element.26), channel_id=1, source_target_pairs={{0,2},{1,3},{2,0},{3,1},{4,6},{5,7},{6,4},{7,5},{8,10},{9,11},{10,... | collective-permute-start | bytes 196616 | tf_op jit(solution)/shard_map/ppermute | solution.py:127
  63.7 10.1 %collective-permute-start.16 = (bf16[256,256]{1,0:T(8,128)(2,1)S(1)}, bf16[256,256]{1,0:T(8,128)(2,1)S(1)}, u32[]{:S(2)}, u32[]{:S(2)}) collective-permute-start(bf16[256,256]{1,0:T(8,128)(2,1)S(1)} %get-tuple-element.32), channel_id=1, source_target_pairs={{0,2},{1,3},{2,0},{3,1},{4,6},{5,7},{6,4},{7,5},{8,10},{9,11},{10,... | collective-permute-start | bytes 393224 | tf_op jit(solution)/shard_map/ppermute | solution.py:127
  74.7 4.3 %collective-permute-start.19 = (bf16[128,256]{0,1:T(8,128)(2,1)S(1)}, bf16[128,256]{0,1:T(8,128)(2,1)S(1)}, u32[]{:S(2)}, u32[]{:S(2)}) collective-permute-start(bf16[128,256]{0,1:T(8,128)(2,1)S(1)} %get-tuple-element.40), channel_id=1, source_target_pairs={{0,1},{1,0},{2,3},{3,2},{4,5},{5,4},{6,7},{7,6},{8,9},{9,8},{10,11... | collective-permute-start | bytes 196616 | tf_op jit(solution)/shard_map/ppermute | solution.py:127
